TPU v7x, 256 devices: a whole 4x4x8 slice. The times are simulated.
256 devices in a mesh: vox: 128 (over x, z, y), sub: 2 (over core).
Axes of the slice: x: 4, y: 4, z: 8, core: 2. Of those that a mesh axis runs over, the one named last changes fastest.
Arguments:
- movie: bfloat16 [262144, 4096], P(('vox', 'sub')), may hold values from -120 to 120
- test_matrix: bfloat16 [4096, 256], replicated, may hold values from -0.09375 to 0.09375
Outputs:
- basis: float32 [262144, 256], P(('vox', 'sub'))
- r_factor: float32 [256, 256], replicated
- projected: float32 [256, 4096], P(None, ('vox', 'sub'))
All inputs are finite; a program needn't handle non-finite values.
Results may differ from a plain program's by a relative error of at most 0.00063.
Values sent between devices are 32-bit elements; how exact they have to be, the bound alone decides.
A program may use at most 128 MiB of HBM per device.

v0:
```python
import jax
import jax.numpy as jnp
from jax import lax
from jax.sharding import PartitionSpec as P


def square_sum(matrix):
    return jnp.dot(matrix.T, matrix, precision=lax.Precision.HIGHEST)


def local(movie, test_matrix):
    sketch = jnp.dot(movie, test_matrix, preferred_element_type=jnp.float32)
    devices_all = lax.axis_size(("vox", "sub"))
    sketch_b = sketch.astype(jnp.bfloat16)
    partial_sum = lax.dot_general(
        sketch_b, movie, (((0,), (0,)), ((), ())), preferred_element_type=jnp.float32
    )
    columns = movie.shape[1] // devices_all
    total = lax.psum(partial_sum, ("vox", "sub"))
    mine = lax.dynamic_slice_in_dim(total, lax.axis_index(("vox", "sub")) * columns, columns, 1)
    gram = lax.psum(square_sum(sketch), ("vox", "sub"))
    lower = jnp.linalg.cholesky(gram)
    width = sketch.shape[1]
    identity = jnp.eye(width, dtype=jnp.float32)
    inverse = lax.linalg.triangular_solve(lower, identity, left_side=True, lower=True)
    scale = jnp.sqrt(jnp.float32(sketch.shape[0] * devices_all))
    basis = jnp.dot(sketch, inverse.T, precision=lax.Precision.HIGHEST) * scale
    projected = jnp.dot(inverse, mine, precision=lax.Precision.HIGHEST)
    return (basis, lower.T / scale, projected)


def solution(mesh):
    placed = (P(("vox", "sub"), None), P())
    return jax.shard_map(
        local,
        mesh=mesh,
        in_specs=placed,
        out_specs=(P(("vox", "sub"), None), P(), P(None, ("vox", "sub"))),
        check_vma=False,
    )
```

profile of v0, /device:TPU:1, one launch (start us, length us, event | category | flops | bytes accessed | tf_op | source)
XLA Modules:
  0.0 379.8 jit_solution(14960276804258986143)
XLA Ops:
  7.2 0.0 all-reduce.4.cloned.1.call-start
  7.2 1.5 copy-done
  8.8 5.9 %fusion.17 = f32[1024,256]{1,0:T(8,128)S(1)} fusion(bf16[1024,4096]{1,0:T(8,128)(2,1)} %param.2, bf16[4096,256]{1,0:T(8,128)(2,1)S(1)} %copy-done), kind=kOutput, calls=%fused_computation.40 | convolution fusion | flops 2147483648 | bytes 11534336 | tf_op jit(solution)/shard_map/dot_general | solution.py:12
  14.6 4.3 %fusion = f32[256,4096]{1,0:T(8,128)} fusion(bf16[1024,4096]{1,0:T(8,128)(2,1)S(1)} %copy-done.1, f32[1024,256]{1,0:T(8,128)S(1)} %fusion.17), kind=kOutput, calls=%fused_computation.5 | convolution fusion | flops 2147745792 | bytes 13631488 | tf_op jit(solution)/shard_map/dot_general | solution.py:15
  19.0 2.5 fusion.18
  21.5 0.0 all-reduce.4.cloned.1.call-update
  21.6 0.6 iota_compare_fusion
  22.2 273.2 %all-reduce.4.cloned.1.call-done = (f32[256,256]{0,1:T(8,128)}, f32[256,4096]{1,0:T(8,128)}) async-done(((f32[256,256]{0,1:T(8,128)}, f32[256,4096]{1,0:T(8,128)}), (f32[256,256]{0,1:T(8,128)}, f32[256,4096]{1,0:T(8,128)})) %all-reduce.4.cloned.1.call-update) | async-done | bytes 4456464 | tf_op jit(solution)/shard_map/psum | solution.py:21
  295.4 1.1 copy.6
  296.5 1.0 fusion.2
  297.5 0.7 copy-done.3
  298.2 11.7 %cholesky.50 = f32[128,128]{1,0:T(8,128)S(1)} custom-call(f32[128,128]{1,0:T(8,128)S(1)} %cholesky.118), custom_call_target="Cholesky" | custom-call | tf_op jit(solution)/shard_map/jit(cholesky)/cholesky | solution.py:22
  310.0 9.8 %custom-call.14 = f32[1,128,128]{1,2,0:T(8,128)S(1)} custom-call(f32[1,128,128]{2,1,0:T(8,128)S(1)} %get-tuple-element.31), custom_call_target="InvertDiagBlocksLowerTriangular" | custom-call | tf_op jit(solution)/shard_map/jit(cholesky)/cholesky | solution.py:22
  319.8 0.2 cholesky.113
  320.0 1.0 constant_dynamic-update-slice_fusion
  321.0 1.1 convolution_subtract_fusion.1
  322.1 11.7 %cholesky.105 = f32[128,128]{1,0:T(8,128)S(1)} custom-call(f32[128,128]{1,0:T(8,128)S(1)} %convolution_subtract_fusion.1), custom_call_target="Cholesky" | custom-call | tf_op jit(solution)/shard_map/jit(cholesky)/cholesky | solution.py:22
  333.9 0.7 compare_reduce_fusion
  335.9 1.7 multiply_bitcast_fusion
  337.6 0.1 triangular_solve.63
  337.6 5.2 %while.1 = (s32[]{:T(128)}, f32[256,256]{1,0:T(8,128)S(1)}, s32[2,2]{1,0:T(2,128)S(1)}, f32[2,128,128]{2,1,0:T(8,128)}, s32[]{:T(128)}) while((s32[]{:T(128)}, f32[256,256]{1,0:T(8,128)S(1)}, s32[2,2]{1,0:T(2,128)S(1)}, f32[2,128,128]{2,1,0:T(8,128)}, s32[]{:T(128)}) %tuple.29), condition=%wide.while_cond, body=%wide.while_body.sunk | while | flops 2 | bytes 132705 | solution.py:25
  337.7 0.6 fusion.30
  338.2 2.0 bitcast_dynamic-update-slice_fusion.2
  340.2 0.6 fusion.30
  340.8 2.0 bitcast_dynamic-update-slice_fusion.2
  342.8 21.1 %custom-call.15 = f32[2,128,128]{1,2,0:T(8,128)} custom-call(f32[2,128,128]{2,1,0:T(8,128)} %get-tuple-element.10), custom_call_target="InvertDiagBlocksLowerTriangular" | custom-call | tf_op jit(solution)/shard_map/triangular_solve | solution.py:25
  363.9 1.1 fusion.6
  365.1 1.0 convolution_subtract_fusion
  366.1 1.2 fusion.9
  367.2 2.0 convolution_multiply_fusion
  369.2 1.8 copy.7
  371.0 1.9 fusion.4
  (13 shorter events, 0.1 us)
Async XLA Ops:
  7.2 1.6 copy-start
  7.2 288.2 %all-reduce.4.cloned.1.call-start = ((), (), s32[]{:S(2)}) async-start(), calls=%async_computation | async-start | bytes 8912896 | tf_op jit(solution)/shard_map/psum | solution.py:21
  8.8 5.9 %copy-start.1 = (bf16[1024,4096]{1,0:T(8,128)(2,1)S(1)}, bf16[1024,4096]{1,0:T(8,128)(2,1)}, u32[]{:S(2)}) copy-start(bf16[1024,4096]{1,0:T(8,128)(2,1)} %param.2) | copy-start | bytes 25165828
  297.5 0.7 copy-start.3
  333.9 2.0 copy-start.2
Sparse Core Ops, SparseCore 0:
  21.6 273.7 all-reduce.3
where the time goes:
time: 381 us; the launch traced here: 380 us
  waiting for transfers between devices  273 us (72%)
  other arithmetic  58.5 us (15%)
  matrix products  22.1 us (6%)
  between operations  15.4 us (4%)
  local copies, waits for them, and re-layouts  10.6 us (3%)
    psum x1, waiting for transfers between devices, local(): gram = lax.psum(square_sum(sketch), ('vox', 'sub'))  273 us
    another operation x6, other arithmetic, local(): lower = jnp.linalg.cholesky(gram)  34 us
    another operation x2, other arithmetic, local(): lax.linalg.triangular_solve(lower, identity, left_side=True, lower=True)  21.1 us
  transfers between devices with their start and end apart: 1, of which 1 were waited for; matrix products, arithmetic and copies ran while one was open for 0% of the time, Pallas kernels for 0%

commit v1 on v0

v1 whole, which is shorter than its diff:
```python
import jax
import jax.numpy as jnp
from jax import lax
from jax.experimental import pallas as pl
from jax.experimental.pallas import tpu as pltpu
from jax.sharding import PartitionSpec as P

F = jnp.float32
HI = lax.Precision.HIGHEST
MESH = pl.DeviceIdType.MESH
VMEM = pltpu.VMEM
DMA = pltpu.SemaphoreType.DMA
NX, NZ, NY = 4, 8, 4
CHUNKS, WIDE = 8, 512


def place(x, z, y, s):
    return ((x * NZ + z) * NY + y, s)


def remote(src, dst, send, recv, device):
    return pltpu.make_async_remote_copy(
        src_ref=src, dst_ref=dst, send_sem=send, recv_sem=recv, device_id=device, device_id_type=MESH
    )


def each(lo, hi, body):
    lax.fori_loop(lo, hi, lambda i, c: (body(i), c)[1], 0)


def factor64(block, left):
    lane = lax.broadcasted_iota(jnp.int32, (8, 128), 1)
    sub = lax.broadcasted_iota(jnp.int32, (8, 128), 0)
    here = (lane < 64) if left else (lane >= 64)
    at, eye = (0, 64) if left else (64, 0)
    rows = [jnp.where(here, block[8 * v:8 * v + 8, :], (lane == eye + 8 * v + sub).astype(F)) for v in range(8)]
    pivots = []
    for p in range(8):
        first = at + 8 * p
        cols = [[jnp.broadcast_to(rows[v][:, first + j:first + j + 1], (8, 128)) for v in range(p, 8)] for j in range(8)]
        pivot = jnp.ones((8, 128), F)
        for k in range(8):
            d = jnp.broadcast_to(cols[k][0][k:k + 1, :], (8, 128))
            pivot = jnp.where(sub == k, d, pivot)
            r = 1.0 / d
            m = [c * r for c in cols[k]]
            m[0] = jnp.where(sub > k, m[0], 0.0)
            row = jnp.broadcast_to(rows[p][k:k + 1, :], (8, 128))
            for j in range(k + 1, 8):
                u = jnp.broadcast_to(cols[j][0][k:k + 1, :], (8, 128))
                cols[j] = [c - a * u for c, a in zip(cols[j], m)]
            for v in range(p, 8):
                rows[v] = rows[v] - m[v - p] * row
        pivots.append(pivot)
    out = [lax.rsqrt(d) * r for d, r in zip(pivots, rows)]
    keep = [jnp.where(here & (lane - at < 8 * v + sub), 0.0, out[v]) for v in range(8)]
    return jnp.concatenate(keep, axis=0)


def factor256(t_ref, diag_ref):
    col = lax.broadcasted_iota(jnp.int32, (64, 256), 1)
    row64 = lax.broadcasted_iota(jnp.int32, (64, 256), 0)
    for s in range(4):
        r0 = 64 * s
        tile = 128 * (s // 2)
        left = s % 2 == 0
        t = t_ref[r0:r0 + 64, :]
        both = factor64(t[:, tile:tile + 128], left)
        diag_ref[r0:r0 + 64, :] = both
        y = jnp.where((col >= r0) & (col < r0 + 64), (col - r0 == row64).astype(F), t)
        z = jnp.zeros((64, 256), F)
        us = jnp.dot(both, jnp.concatenate([z, y] if left else [y, z], axis=0), precision=HI, preferred_element_type=F)
        t_ref[r0:r0 + 64, :] = us
        if s < 3:
            full = lax.dot_general(us, us, (((0,), (0,)), ((), ())), precision=HI, preferred_element_type=F)
            colr = lax.broadcasted_iota(jnp.int32, (192 - r0, 256), 1)
            rest = t_ref[r0 + 64:, :]
            t_ref[r0 + 64:, :] = jnp.where((colr >= r0) & (colr < r0 + 64), 0.0, rest) - full[r0 + 64:, :]


def parts(t_ref, diag_ref):
    col = lax.broadcasted_iota(jnp.int32, (256, 256), 1)
    row = lax.broadcasted_iota(jnp.int32, (256, 256), 0)
    t = t_ref[...]
    d = diag_ref[...]
    dd = jnp.concatenate([d, d], axis=1)
    upper = jnp.where(col // 64 == row // 64, dd, t)
    return jnp.where(col >= row, upper, 0.0), jnp.where(col <= row, t, 0.0)


def reduce_kernel(
    movie, test, sketch, gram, cross,
    mv, tv, skt, skb, part, drecv, half, gpart, grs, gz, a_tmp, a_in, b_tmp, b_in, pa, pb, r2, p2, r3,
    msem, tsem, dsend, drsem, gs_send, gs_recv, gz_send, gz_recv, ga_send, ga_recv,
    s1_send, s1_recv, s2_send, s2_recv, s3_send, s3_recv, s4_send, s4_recv,
):
    vox, s = lax.axis_index("vox"), lax.axis_index("sub")
    y = lax.rem(vox, NY)
    z = lax.rem(lax.div(vox, NY), NZ)
    x = lax.div(vox, NY * NZ)
    q = (x * NY + y) * 2 + s
    other = place(x, z, y, 1 - s)

    def load(c):
        wide = pl.ds(pl.multiple_of(c * WIDE, WIDE), WIDE)
        return (
            pltpu.make_async_copy(movie.at[:, wide], mv.at[c], msem.at[c]),
            pltpu.make_async_copy(test.at[wide], tv.at[c], tsem.at[c]),
        )

    def start(c):
        for copy in load(c):
            copy.start()

    each(0, CHUNKS, start)

    def plane(d):
        t = lax.rem(q + d, 32)
        return t, place(lax.div(t, NY * 2), z, lax.rem(lax.div(t, 2), NY), lax.rem(t, 2))

    def column(d):
        t = lax.rem(z + d, NZ)
        return t, place(x, t, y, s)

    barrier = pltpu.get_barrier_semaphore()

    def greet(device):
        pl.semaphore_signal(barrier, inc=1, device_id=device, device_id_type=MESH)

    each(1, 32, lambda d: greet(plane(d)[1]))
    each(1, NZ, lambda d: greet(column(d)[1]))

    sketch[...] = jnp.zeros_like(sketch)

    def project(c):
        for copy in load(c):
            copy.wait()
        sketch[...] += jnp.dot(mv[c], tv[c], preferred_element_type=F)

    each(0, CHUNKS, project)
    skt[...] = jnp.transpose(sketch[...])
    skb[...] = skt[...].astype(jnp.bfloat16)
    gpart[...] = jnp.dot(skt[...], sketch[...], precision=HI, preferred_element_type=F).reshape(32, 8, 256)

    pl.semaphore_wait(barrier, 31 + NZ - 1)

    def gram_scatter(d):
        t, device = plane(d)
        return remote(gpart.at[t], grs.at[d], gs_send.at[d], gs_recv.at[d], device)

    each(1, 32, lambda d: gram_scatter(d).start())

    def across(c):
        rows = pl.ds(pl.multiple_of((1 - s) * 128, 128), 128)
        return remote(part.at[c, rows], drecv.at[c], dsend.at[c], drsem.at[c], other)

    def multiply(c):
        part[c] = jnp.dot(skb[...], mv[c], preferred_element_type=F)
        across(c).start()

    each(0, CHUNKS, multiply)

    each(1, 32, lambda d: gram_scatter(d).wait_recv())
    total = gpart[q]
    for d in range(1, 32):
        total = total + grs[d]
    gz[z] = total

    def gram_column(d):
        t, device = column(d)
        return remote(gz.at[z], gz.at[z], gz_send.at[d], gz_recv.at[d], device)

    def gram_column_from(d):
        t = lax.rem(z - d + NZ, NZ)
        return remote(gz.at[t], gz.at[t], gz_send.at[d], gz_recv.at[d], place(x, t, y, s))

    each(1, NZ, lambda d: gram_column(d).start())

    def fold(c):
        across(c).wait_recv()
        half[c] = part[c, pl.ds(pl.multiple_of(s * 128, 128), 128)] + drecv[c]

    each(0, CHUNKS, fold)

    xr, xo, xl = (lax.rem(x + d, NX) for d in (1, 2, 3))
    yr, yo, yl = (lax.rem(y + d, NY) for d in (1, 2, 3))
    right_x, left_x = place(xr, z, y, s), place(xl, z, y, s)
    right_y, left_y = place(x, z, yr, s), place(x, z, yl, s)

    def rows(i):
        return pl.ds(pl.multiple_of(i * 32, 32), 32)

    def ring(i, src, dst, device):
        return remote(src, dst, s1_send.at[i], s1_recv.at[i], device)

    ring_a = [
        ring(0, half.at[2 * xo], a_tmp.at[0], right_x),
        ring(1, half.at[2 * xo + 1], a_tmp.at[1], left_x),
        ring(2, half.at[2 * xr + 1], a_in.at[0, 1], right_x),
        ring(3, half.at[2 * xl], a_in.at[1, 0], left_x),
        ring(4, half.at[2 * xr], a_in.at[0, 0], right_x),
        ring(5, half.at[2 * xl + 1], a_in.at[1, 1], left_x),
    ]
    lo, hi = pl.ds(0, 4), pl.ds(4, 4)
    ring_b = [
        ring(0, half.at[lo, rows(yo)], b_tmp.at[0], right_y),
        ring(1, half.at[hi, rows(yo)], b_tmp.at[1], left_y),
        ring(2, half.at[hi, rows(yr)], b_in.at[0, hi], right_y),
        ring(3, half.at[lo, rows(yl)], b_in.at[1, lo], left_y),
        ring(4, half.at[lo, rows(yr)], b_in.at[0, lo], right_y),
        ring(5, half.at[hi, rows(yl)], b_in.at[1, hi], left_y),
    ]

    @pl.when(s == 0)
    def _():
        for copy in ring_a[:4]:
            copy.start()

    @pl.when(s == 1)
    def _():
        for copy in ring_b[:4]:
            copy.start()

    each(1, NZ, lambda d: gram_column_from(d).wait_recv())
    each(1, NZ, lambda d: gram_column(d).wait_send())
    total = gz[0]
    for j in range(1, NZ):
        total = total + gz[j]
    gram[q] = total

    def gram_gather(d):
        t, device = plane(d)
        return remote(gram.at[q], gram.at[q], ga_send.at[d], ga_recv.at[d], device)

    def gram_gather_from(d):
        t, device = plane(32 - d)
        return remote(gram.at[t], gram.at[t], ga_send.at[d], ga_recv.at[d], device)

    each(1, 32, lambda d: gram_gather(d).start())

    @pl.when(s == 0)
    def _():
        ring_a[0].wait_recv()
        half[2 * xr] = half[2 * xr] + a_tmp[0]
        ring_a[4].start()
        ring_a[1].wait_recv()
        half[2 * xl + 1] = half[2 * xl + 1] + a_tmp[1]
        ring_a[5].start()
        for copy in ring_a[2:]:
            copy.wait_recv()
        pa[...] = half[pl.ds(2 * x, 2)] + a_in[0] + a_in[1]

    @pl.when(s == 1)
    def _():
        ring_b[0].wait_recv()
        half[lo, rows(yr)] = half[lo, rows(yr)] + b_tmp[0]
        ring_b[4].start()
        ring_b[1].wait_recv()
        half[hi, rows(yl)] = half[hi, rows(yl)] + b_tmp[1]
        ring_b[5].start()
        for copy in ring_b[2:]:
            copy.wait_recv()
        pb[...] = half[:, rows(y)] + b_in[0] + b_in[1]

    def second_a(d):
        t = (yr, yo, yl)[d]
        return remote(pa.at[:, rows(t)], r2.at[d], s2_send.at[d], s2_recv.at[d], place(x, z, t, s))

    def second_b(d):
        t = (xr, xo, xl)[d]
        return remote(pb.at[pl.ds(2 * t, 2)], r2.at[d], s2_send.at[d], s2_recv.at[d], place(t, z, y, s))

    @pl.when(s == 0)
    def _():
        for d in range(3):
            second_a(d).start()
        for d in range(3):
            second_a(d).wait_recv()
        p2[...] = pa[:, rows(y)] + r2[0] + r2[1] + r2[2]

    @pl.when(s == 1)
    def _():
        for d in range(3):
            second_b(d).start()
        for d in range(3):
            second_b(d).wait_recv()
        p2[...] = pb[pl.ds(2 * x, 2)] + r2[0] + r2[1] + r2[2]

    def tile(t):
        return lax.div(t, 4), slice(None), pl.ds(pl.multiple_of(lax.rem(t, 4) * 128, 128), 128)

    def third(d):
        t, device = column(d)
        return remote(p2.at[tile(t)], r3.at[d], s3_send.at[d], s3_recv.at[d], device)

    each(1, NZ, lambda d: third(d).start())
    each(1, NZ, lambda d: third(d).wait_recv())
    total = p2[tile(z)]
    for d in range(1, NZ):
        total = total + r3[d]
    cross[rows(s * 4 + y)] = total

    def fourth(d):
        t = lax.rem(s * 4 + y + d, 8)
        mine = cross.at[rows(s * 4 + y)]
        return remote(mine, mine, s4_send.at[d], s4_recv.at[d], place(x, z, lax.rem(t, 4), lax.div(t, 4)))

    def fourth_from(d):
        t = lax.rem(s * 4 + y - d + 8, 8)
        here = cross.at[rows(t)]
        return remote(here, here, s4_send.at[d], s4_recv.at[d], place(x, z, lax.rem(t, 4), lax.div(t, 4)))

    each(1, 8, lambda d: fourth(d).start())
    each(1, 8, lambda d: fourth_from(d).wait_recv())
    each(1, 32, lambda d: gram_gather_from(d).wait_recv())

    each(1, 32, lambda d: gram_scatter(d).wait_send())
    each(1, 32, lambda d: gram_gather(d).wait_send())
    each(0, CHUNKS, lambda c: across(c).wait_send())
    each(1, NZ, lambda d: third(d).wait_send())
    each(1, 8, lambda d: fourth(d).wait_send())

    @pl.when(s == 0)
    def _():
        for copy in ring_a:
            copy.wait_send()
        for d in range(3):
            second_a(d).wait_send()

    @pl.when(s == 1)
    def _():
        for copy in ring_b:
            copy.wait_send()
        for d in range(3):
            second_b(d).wait_send()


def finish_kernel(voxels, sketch, gram, cross, basis, r_factor, projected, t_ref, diag_ref):
    t_ref[...] = gram[...]
    factor256(t_ref, diag_ref)
    upper, inverse = parts(t_ref, diag_ref)
    scale = jnp.sqrt(F(voxels))
    r_factor[...] = upper / scale
    basis[...] = jnp.dot(sketch[...], jnp.transpose(inverse), precision=HI, preferred_element_type=F) * scale
    full = jnp.dot(inverse, cross[...], precision=HI, preferred_element_type=F)
    first = (lax.rem(lax.axis_index("vox"), NY) * 2 + lax.axis_index("sub")) * 16
    projected[...] = pltpu.roll(full, lax.rem(128 - first, 128), 1)[:, :16]


def local(movie, test_matrix):
    shape = jax.ShapeDtypeStruct
    in_vmem = pl.BlockSpec(memory_space=VMEM)
    sketch, gram, cross = pl.pallas_call(
        reduce_kernel,
        out_shape=(shape((1024, 256), F), shape((32, 8, 256), F), shape((256, 128), F)),
        in_specs=[pl.BlockSpec(memory_space=pl.ANY)] * 2,
        out_specs=[in_vmem] * 3,
        scratch_shapes=[
            VMEM((CHUNKS, 1024, WIDE), jnp.bfloat16),
            VMEM((CHUNKS, WIDE, 256), jnp.bfloat16),
            VMEM((256, 1024), F),
            VMEM((256, 1024), jnp.bfloat16),
            VMEM((CHUNKS, 256, WIDE), F),
            VMEM((CHUNKS, 128, WIDE), F),
            VMEM((CHUNKS, 128, WIDE), F),
            VMEM((32, 8, 256), F),
            VMEM((32, 8, 256), F),
            VMEM((NZ, 8, 256), F),
            VMEM((2, 128, WIDE), F),
            VMEM((2, 2, 128, WIDE), F),
            VMEM((2, 4, 32, WIDE), F),
            VMEM((2, 8, 32, WIDE), F),
            VMEM((2, 128, WIDE), F),
            VMEM((8, 32, WIDE), F),
            VMEM((3, 2, 32, WIDE), F),
            VMEM((2, 32, WIDE), F),
            VMEM((NZ, 32, 128), F),
        ]
        + [DMA((n,)) for n in (8, 8, 8, 8, 32, 32, 8, 8, 32, 32, 6, 6, 3, 3, 8, 8, 8, 8)],
        compiler_params=pltpu.CompilerParams(
            collective_id=0, has_side_effects=True, vmem_limit_bytes=60 * 1024 * 1024
        ),
    )(movie, test_matrix)
    voxels = movie.shape[0] * NX * NY * NZ * 2
    return pl.pallas_call(
        lambda *refs: finish_kernel(voxels, *refs),
        out_shape=(shape((1024, 256), F), shape((256, 256), F), shape((256, 16), F)),
        in_specs=[in_vmem] * 3,
        out_specs=[in_vmem] * 3,
        scratch_shapes=[VMEM((256, 256), F), VMEM((256, 128), F)],
    )(sketch, gram.reshape(256, 256), cross)


def solution(mesh):
    placed = (P(("vox", "sub"), None), P())
    return jax.shard_map(
        local,
        mesh=mesh,
        in_specs=placed,
        out_specs=(P(("vox", "sub"), None), P(), P(None, ("vox", "sub"))),
        check_vma=False,
    )
```

time: 381 us -> 68.7 us (0.18)
  waiting for transfers between devices: 273 us -> 0 us
  Pallas kernels: 0 us -> 66.3 us
  other arithmetic: 58.5 us -> 0 us
  matrix products: 22.1 us -> 0 us
  between operations: 15.4 us -> 0.64 us
  local copies, waits for them, and re-layouts: 10.6 us -> 1.58 us
    psum x1 -> x0, waiting for transfers between devices: 273 us -> none  [local(): gram = lax.psum(square_sum(sketch), ('vox', 'sub'))]
    pallas_call x0 -> x2, Pallas kernels: none -> 66.3 us  [the longest x1 53.4 us: local(): pl.pallas_call(reduce_kernel, out_shape=(shape((1024, 256), F), shape((32...]
    another operation x8 -> x0, other arithmetic: 55.1 us -> none  [the longest x6 34 us: local(): lower = jnp.linalg.cholesky(gram)]
    dot_general x5 -> x0, matrix products: 16.7 us -> none  [the longest x1 5.86 us: local(): sketch = jnp.dot(movie, test_matrix, preferred_element_type=jnp.float32)]
    another operation x9 -> x0, local copies, waits for them, and re-layouts: 5.46 us -> none
    another operation x5 -> x0, matrix products: 5.42 us -> none  [the longest x3 3.26 us: local(): lax.linalg.triangular_solve(lower, identity, left_side=True, lower=True)]
    unnamed x9 -> x0, local copies, waits for them, and re-layouts: 4.03 us -> none
  transfers between devices with their start and end apart: 1 -> 0, of which waited for: 1 -> 0; matrix products, arithmetic and copies ran while one was open for 0% -> 0% of each run, Pallas kernels for 0% -> 0%
where the time goes in v1:
time: 68.7 us; the launch traced here: 68.6 us
  Pallas kernels  66.3 us (97%)
  local copies, waits for them, and re-layouts  1.58 us (2%)
    pallas_call x1, Pallas kernels, local(): pl.pallas_call(reduce_kernel, out_shape=(shape((1024, 256), F), shape((32...  53.4 us
    pallas_call x1, Pallas kernels, local(): pl.pallas_call(lambda *refs: finish_kernel(voxels, *refs), out_shape=(sha...  13 us
    pallas_call x1, local copies, waits for them, and re-layouts, local(): pl.pallas_call(lambda *refs: finish_kernel(voxels, *refs), out_shape=(sha...  1.58 us

profile of v1, /device:TPU:1, one launch (start us, length us, event | category | flops | bytes accessed | tf_op | source)
XLA Modules:
  0.0 68.6 jit_solution(6528165765138030881)
XLA Ops:
  0.6 53.4 %shard_map.49 = (f32[1024,256]{1,0:T(8,128)}, f32[32,8,256]{2,1,0:T(8,128)}, f32[256,128]{1,0:T(8,128)}) custom-call(bf16[1024,4096]{1,0:T(8,128)(2,1)} %movie.1, bf16[4096,256]{1,0:T(8,128)(2,1)} %test.1), custom_call_target="tpu_custom_call" | custom-call | tf_op jit(solution)/shard_map/pallas_call | solution.py:353
  54.0 13.0 %shard_map.50 = (f32[1024,256]{1,0:T(8,128)}, f32[256,256]{1,0:T(8,128)}, f32[256,16]{1,0:T(8,128)}) custom-call(f32[1024,256]{1,0:T(8,128)} %get-tuple-element.6.refs_0_, f32[256,256]{1,0:T(8,128)} %bitcast.1, f32[256,128]{1,0:T(8,128)} %get-tuple-element.8.refs_2_), custom_call_target="tpu_custom_call" | custom-call | tf_op jit(solution)/shard_map/pallas_call | solution.py:385
  67.0 1.6 %copy.5 = f32[256,16]{0,1:T(8,128)} copy(f32[256,16]{1,0:T(8,128)} %get-tuple-element.11) | data formatting | bytes 32768 | tf_op jit(solution)/shard_map/pallas_call | solution.py:385

commit v2 on v1

v2 whole, which is shorter than its diff:
```python
import jax
import jax.numpy as jnp
from jax import lax
from jax.experimental import pallas as pl
from jax.experimental.pallas import tpu as pltpu
from jax.sharding import PartitionSpec as P

F = jnp.float32
HI = lax.Precision.HIGHEST
MESH = pl.DeviceIdType.MESH
VMEM = pltpu.VMEM
DMA = pltpu.SemaphoreType.DMA
NX, NZ, NY = 4, 8, 4
CHUNKS, WIDE = 8, 512


def place(x, z, y, s):
    return ((x * NZ + z) * NY + y, s)


def remote(src, dst, send, recv, device):
    return pltpu.make_async_remote_copy(
        src_ref=src, dst_ref=dst, send_sem=send, recv_sem=recv, device_id=device, device_id_type=MESH
    )


def each(lo, hi, body):
    lax.fori_loop(lo, hi, lambda i, c: (body(i), c)[1], 0)


def factor64(block, left):
    lane = lax.broadcasted_iota(jnp.int32, (8, 8, 128), 2)
    line = lax.broadcasted_iota(jnp.int32, (8, 8, 128), 0) * 8 + lax.broadcasted_iota(jnp.int32, (8, 8, 128), 1)
    sub = lax.broadcasted_iota(jnp.int32, (8, 128), 0)
    here = (lane < 64) if left else (lane >= 64)
    at, eye = (0, 64) if left else (64, 0)
    below = jnp.where(here, block.reshape(8, 8, 128), (lane == eye + line).astype(F))
    done = []
    for p in range(8):
        n = 8 - p
        first = at + 8 * p
        cols = [jnp.broadcast_to(below[:, :, first + j:first + j + 1], (n, 8, 128)) for j in range(8)]
        pivot = jnp.ones((8, 128), F)
        for k in range(8):
            d = jnp.broadcast_to(cols[k][0, k:k + 1, :], (8, 128))
            pivot = jnp.where(sub == k, d, pivot)
            m = cols[k] * (1.0 / d)[None]
            top = jnp.where(sub > k, m[0], 0.0)[None]
            m = jnp.concatenate([top, m[1:]], axis=0) if n > 1 else top
            row = jnp.broadcast_to(below[0, k:k + 1, :], (8, 128))
            for j in range(k + 1, 8):
                u = jnp.broadcast_to(cols[j][0, k:k + 1, :], (8, 128))
                cols[j] = cols[j] - m * u[None]
            below = below - m * row[None]
        done.append(lax.rsqrt(pivot) * below[0])
        below = below[1:]
    out = jnp.stack(done)
    return jnp.where(here & (lane - at < line), 0.0, out).reshape(64, 128)


def factor_block(t_ref, diag_ref, s):
    col = lax.broadcasted_iota(jnp.int32, (64, 256), 1)
    row = lax.broadcasted_iota(jnp.int32, (64, 256), 0)
    r0 = 64 * s
    tile = 128 * (s // 2)
    left = s % 2 == 0
    t = t_ref[r0 : r0 + 64, :]
    both = factor64(t[:, tile : tile + 128], left)
    diag_ref[r0 : r0 + 64, :] = both
    y = jnp.where((col >= r0) & (col < r0 + 64), (col - r0 == row).astype(F), t)
    z = jnp.zeros((64, 256), F)
    us = jnp.dot(both, jnp.concatenate([z, y] if left else [y, z], axis=0), precision=HI, preferred_element_type=F)
    t_ref[r0 : r0 + 64, :] = us
    if s < 3:
        full = lax.dot_general(us, us, (((0,), (0,)), ((), ())), precision=HI, preferred_element_type=F)
        col = lax.broadcasted_iota(jnp.int32, (192 - r0, 256), 1)
        rest = jnp.where((col >= r0) & (col < r0 + 64), 0.0, t_ref[r0 + 64 :, :])
        t_ref[r0 + 64 :, :] = rest - full[r0 + 64 :, :]


def parts(t_ref, diag_ref):
    col = lax.broadcasted_iota(jnp.int32, (256, 256), 1)
    row = lax.broadcasted_iota(jnp.int32, (256, 256), 0)
    t = t_ref[...]
    d = diag_ref[...]
    dd = jnp.concatenate([d, d], axis=1)
    upper = jnp.where(col // 64 == row // 64, dd, t)
    return jnp.where(col >= row, upper, 0.0), jnp.where(col <= row, t, 0.0)


def reduce_kernel(
    movie, test, sketch, upper, inverse, cross,
    mv, tv, skt, skb, part, drecv, half, gpart, grs, gz, gram, t_ref, diag_ref,
    a_tmp, a_in, b_tmp, b_in, pa, pb, r2, p2, r3, p3,
    msem, tsem, dsend, drsem, gs_send, gs_recv, gz_send, gz_recv, ga_send, ga_recv,
    s1_send, s1_recv, s2_send, s2_recv, s3_send, s3_recv, s4_send, s4_recv,
):
    vox, s = lax.axis_index("vox"), lax.axis_index("sub")
    y = lax.rem(vox, NY)
    z = lax.rem(lax.div(vox, NY), NZ)
    x = lax.div(vox, NY * NZ)
    q = (x * NY + y) * 2 + s
    other = place(x, z, y, 1 - s)

    def load(c):
        wide = pl.ds(pl.multiple_of(c * WIDE, WIDE), WIDE)
        return (
            pltpu.make_async_copy(movie.at[:, wide], mv.at[c], msem.at[c]),
            pltpu.make_async_copy(test.at[wide], tv.at[c], tsem.at[c]),
        )

    def start(c):
        for copy in load(c):
            copy.start()

    each(0, CHUNKS, start)

    def plane(d):
        t = lax.rem(q + d, 32)
        return t, place(lax.div(t, NY * 2), z, lax.rem(lax.div(t, 2), NY), lax.rem(t, 2))

    def column(d):
        t = lax.rem(z + d, NZ)
        return t, place(x, t, y, s)

    barrier = pltpu.get_barrier_semaphore()

    def greet(device):
        pl.semaphore_signal(barrier, inc=1, device_id=device, device_id_type=MESH)

    each(1, 32, lambda d: greet(plane(d)[1]))
    each(1, NZ, lambda d: greet(column(d)[1]))

    sketch[...] = jnp.zeros_like(sketch)

    def project(c):
        for copy in load(c):
            copy.wait()
        sketch[...] += jnp.dot(mv[c], tv[c], preferred_element_type=F)

    each(0, CHUNKS, project)
    skt[...] = jnp.transpose(sketch[...])
    skb[...] = skt[...].astype(jnp.bfloat16)
    gpart[...] = jnp.dot(skt[...], sketch[...], precision=HI, preferred_element_type=F).reshape(32, 8, 256)

    pl.semaphore_wait(barrier, 31 + NZ - 1)

    def gram_scatter(d):
        t, device = plane(d)
        return remote(gpart.at[t], grs.at[d], gs_send.at[d], gs_recv.at[d], device)

    each(1, 32, lambda d: gram_scatter(d).start())

    xr, xo, xl = (lax.rem(x + d, NX) for d in (1, 2, 3))
    yr, yo, yl = (lax.rem(y + d, NY) for d in (1, 2, 3))
    right_x, left_x = place(xr, z, y, s), place(xl, z, y, s)
    right_y, left_y = place(x, z, yr, s), place(x, z, yl, s)

    def across(i):
        rows = pl.ds(pl.multiple_of((1 - s) * 128, 128), 128)
        return remote(part.at[i, rows], drecv.at[i], dsend.at[i], drsem.at[i], other)

    def multiply(i):
        part[i] = jnp.dot(skb[...], mv[lax.rem(2 * xo + i, CHUNKS)], preferred_element_type=F)
        across(i).start()

    each(0, CHUNKS, multiply)

    def ring(i, src, dst, device):
        return remote(src, dst, s1_send.at[i], s1_recv.at[i], device)

    lo, hi = pl.ds(0, 4), pl.ds(4, 4)
    ring_a = [
        ring(0, half.at[0, lo], a_tmp.at[0], right_x),
        ring(1, half.at[0, hi], a_tmp.at[1], left_x),
        ring(2, half.at[3, hi], a_in.at[0, hi], right_x),
        ring(3, half.at[1, lo], a_in.at[1, lo], left_x),
        ring(4, half.at[3, lo], a_in.at[0, lo], right_x),
        ring(5, half.at[1, hi], a_in.at[1, hi], left_x),
    ]
    be, af = pl.ds(0, 2), pl.ds(2, 2)
    every = pl.ds(0, NZ)
    ring_b = [
        ring(0, half.at[be, every, yo], b_tmp.at[0], right_y),
        ring(1, half.at[af, every, yo], b_tmp.at[1], left_y),
        ring(2, half.at[af, every, yr], b_in.at[0, af], right_y),
        ring(3, half.at[be, every, yl], b_in.at[1, be], left_y),
        ring(4, half.at[be, every, yr], b_in.at[0, be], right_y),
        ring(5, half.at[af, every, yl], b_in.at[1, af], left_y),
    ]

    def begin(a, b):
        @pl.when(s == 0)
        def _():
            for i in a:
                ring_a[i].start()

        @pl.when(s == 1)
        def _():
            for i in b:
                ring_b[i].start()

    after = {1: ((0, 1), ()), 3: ((3,), (0, 3)), 7: ((2,), (1, 2))}
    for i in range(CHUNKS):
        across(i).wait_recv()
        both = part[i, pl.ds(pl.multiple_of(s * 128, 128), 128)] + drecv[i]
        half[i // 2, pl.ds(4 * (i % 2), 4)] = jnp.transpose(both).reshape(4, NY, 32, 128)
        if i in after:
            begin(*after[i])

    each(1, 32, lambda d: gram_scatter(d).wait_recv())
    total = gpart[q]
    for d in range(1, 32):
        total = total + grs[d]
    gz[z] = total

    def gram_column(d):
        t, device = column(d)
        return remote(gz.at[z], gz.at[z], gz_send.at[d], gz_recv.at[d], device)

    def gram_column_from(d):
        t = lax.rem(z - d + NZ, NZ)
        return remote(gz.at[t], gz.at[t], gz_send.at[d], gz_recv.at[d], place(x, t, y, s))

    each(1, NZ, lambda d: gram_column(d).start())

    @pl.when(s == 0)
    def _():
        ring_a[0].wait_recv()
        half[3, lo] = half[3, lo] + a_tmp[0]
        ring_a[4].start()
        ring_a[1].wait_recv()
        half[1, hi] = half[1, hi] + a_tmp[1]
        ring_a[5].start()

    @pl.when(s == 1)
    def _():
        ring_b[0].wait_recv()
        half[be, every, yr] = half[be, every, yr] + b_tmp[0]
        ring_b[4].start()
        ring_b[1].wait_recv()
        half[af, every, yl] = half[af, every, yl] + b_tmp[1]
        ring_b[5].start()

    each(1, NZ, lambda d: gram_column_from(d).wait_recv())
    each(1, NZ, lambda d: gram_column(d).wait_send())
    total = gz[0]
    for j in range(1, NZ):
        total = total + gz[j]
    gram[q] = total

    def gram_gather(d):
        t, device = plane(d)
        return remote(gram.at[q], gram.at[q], ga_send.at[d], ga_recv.at[d], device)

    def gram_gather_from(d):
        t, device = plane(32 - d)
        return remote(gram.at[t], gram.at[t], ga_send.at[d], ga_recv.at[d], device)

    each(1, 32, lambda d: gram_gather(d).start())

    def second_a(d):
        t = (yr, yo, yl)[d]
        return remote(pa.at[every, t], r2.at[d], s2_send.at[d], s2_recv.at[d], place(x, z, t, s))

    def second_b(d):
        t = (xr, xo, xl)[d]
        return remote(pb.at[(3, 0, 1)[d]], r2.at[d], s2_send.at[d], s2_recv.at[d], place(t, z, y, s))

    @pl.when(s == 0)
    def _():
        for copy in ring_a[2:]:
            copy.wait_recv()
        pa[...] = half[2] + a_in[0] + a_in[1]
        for d in range(3):
            second_a(d).start()

    @pl.when(s == 1)
    def _():
        for copy in ring_b[2:]:
            copy.wait_recv()
        pb[...] = half[:, :, y] + b_in[0] + b_in[1]
        for d in range(3):
            second_b(d).start()

    each(1, 32, lambda d: gram_gather_from(d).wait_recv())
    t_ref[...] = gram[...].reshape(256, 256)
    factor_block(t_ref, diag_ref, 0)

    for d in range(3):
        second_a(d).wait_recv()

    @pl.when(s == 0)
    def _():
        p2[...] = pa[:, y] + r2[0] + r2[1] + r2[2]

    @pl.when(s == 1)
    def _():
        p2[...] = pb[2] + r2[0] + r2[1] + r2[2]

    def third(d):
        t, device = column(d)
        return remote(p2.at[t], r3.at[d], s3_send.at[d], s3_recv.at[d], device)

    each(1, NZ, lambda d: third(d).start())
    for block in range(1, 4):
        factor_block(t_ref, diag_ref, block)
    upper[...], inverse[...] = parts(t_ref, diag_ref)

    each(1, NZ, lambda d: third(d).wait_recv())
    total = p2[z]
    for d in range(1, NZ):
        total = total + r3[d]
    p3[...] = total.reshape(2, 16, 128)
    last = remote(p3.at[1 - s], cross.at[s], s4_send.at[0], s4_recv.at[0], other)
    last.start()
    cross[s] = p3[s]
    remote(p3.at[s], cross.at[1 - s], s4_send.at[0], s4_recv.at[0], other).wait_recv()

    each(1, 32, lambda d: gram_scatter(d).wait_send())
    each(1, 32, lambda d: gram_gather(d).wait_send())
    each(0, CHUNKS, lambda i: across(i).wait_send())
    each(1, NZ, lambda d: third(d).wait_send())
    last.wait_send()

    @pl.when(s == 0)
    def _():
        for copy in ring_a:
            copy.wait_send()
        for d in range(3):
            second_a(d).wait_send()

    @pl.when(s == 1)
    def _():
        for copy in ring_b:
            copy.wait_send()
        for d in range(3):
            second_b(d).wait_send()


def finish_kernel(voxels, sketch, upper, inverse, cross, basis, r_factor, projected):
    scale = jnp.sqrt(F(voxels))
    turned = jnp.transpose(inverse[...])
    r_factor[...] = upper[...] / scale
    basis[...] = jnp.dot(sketch[...], turned, precision=HI, preferred_element_type=F) * scale
    both = jnp.concatenate([cross[0], cross[1]], axis=1)
    projected[...] = jnp.dot(both, turned, precision=HI, preferred_element_type=F)


def local(movie, test_matrix):
    shape = jax.ShapeDtypeStruct
    movie, test_matrix = (pltpu.with_memory_space_constraint(a, pltpu.HBM) for a in (movie, test_matrix))
    in_vmem = pl.BlockSpec(memory_space=VMEM)
    square = shape((256, 256), F)
    sketch, upper, inverse, cross = pl.pallas_call(
        reduce_kernel,
        out_shape=(shape((1024, 256), F), square, square, shape((2, 16, 128), F)),
        in_specs=[pl.BlockSpec(memory_space=pltpu.HBM)] * 2,
        out_specs=[in_vmem] * 4,
        scratch_shapes=[
            VMEM((CHUNKS, 1024, WIDE), jnp.bfloat16),
            VMEM((CHUNKS, WIDE, 256), jnp.bfloat16),
            VMEM((256, 1024), F),
            VMEM((256, 1024), jnp.bfloat16),
            VMEM((CHUNKS, 256, WIDE), F),
            VMEM((CHUNKS, 128, WIDE), F),
            VMEM((NX, NZ, NY, 32, 128), F),
            VMEM((32, 8, 256), F),
            VMEM((32, 8, 256), F),
            VMEM((NZ, 8, 256), F),
            VMEM((32, 8, 256), F),
            VMEM((256, 256), F),
            VMEM((256, 128), F),
            VMEM((2, 4, NY, 32, 128), F),
            VMEM((2, NZ, NY, 32, 128), F),
            VMEM((2, 2, NZ, 32, 128), F),
            VMEM((2, NX, NZ, 32, 128), F),
            VMEM((NZ, NY, 32, 128), F),
            VMEM((NX, NZ, 32, 128), F),
            VMEM((3, NZ, 32, 128), F),
            VMEM((NZ, 32, 128), F),
            VMEM((NZ, 32, 128), F),
            VMEM((2, 16, 128), F),
        ]
        + [DMA((n,)) for n in (8, 8, 8, 8, 32, 32, 8, 8, 32, 32, 6, 6, 3, 3, 8, 8, 1, 1)],
        compiler_params=pltpu.CompilerParams(
            collective_id=0, has_side_effects=True, vmem_limit_bytes=40 * 1024 * 1024
        ),
    )(movie, test_matrix)
    voxels = movie.shape[0] * NX * NY * NZ * 2
    basis, r_factor, projected = pl.pallas_call(
        lambda *refs: finish_kernel(voxels, *refs),
        out_shape=(shape((1024, 256), F), square, shape((16, 256), F)),
        in_specs=[in_vmem] * 4,
        out_specs=[in_vmem] * 3,
        compiler_params=pltpu.CompilerParams(vmem_limit_bytes=16 * 1024 * 1024),
    )(sketch, upper, inverse, cross)
    return basis, r_factor, projected.T


def solution(mesh):
    placed = (P(("vox", "sub"), None), P())
    return jax.shard_map(
        local,
        mesh=mesh,
        in_specs=placed,
        out_specs=(P(("vox", "sub"), None), P(), P(None, ("vox", "sub"))),
        check_vma=False,
    )
```

time: 68.7 us -> 49.7 us (0.72)
  Pallas kernels: 66.3 us -> 49 us
  local copies, waits for them, and re-layouts: 1.58 us -> 0 us
    pallas_call x1, Pallas kernels: 13 us -> 2.21 us  [local(): pl.pallas_call(lambda *refs: finish_kernel(voxels, *refs), out_shape=(sha...]
    pallas_call x1, Pallas kernels: 53.4 us -> 46.8 us  [local(): pl.pallas_call(reduce_kernel, out_shape=(shape((1024, 256), F), square, s...]
    pallas_call x1 -> x0, local copies, waits for them, and re-layouts: 1.58 us -> none  [local(): pl.pallas_call(lambda *refs: finish_kernel(voxels, *refs), out_shape=(sha...]
where the time goes in v2:
time: 49.7 us; the launch traced here: 49.6 us
  Pallas kernels  49 us (99%)
  between operations  0.64 us (1%)
    pallas_call x1, Pallas kernels, local(): pl.pallas_call(reduce_kernel, out_shape=(shape((1024, 256), F), square, s...  46.8 us
    pallas_call x1, Pallas kernels, local(): pl.pallas_call(lambda *refs: finish_kernel(voxels, *refs), out_shape=(sha...  2.21 us

profile of v2, /device:TPU:1, one launch (start us, length us, event | category | flops | bytes accessed | tf_op | source)
XLA Modules:
  0.0 49.6 jit_solution(324353750765023687)
XLA Ops:
  0.6 46.8 %shard_map.49 = (f32[1024,256]{1,0:T(8,128)S(1)}, f32[256,256]{1,0:T(8,128)S(1)}, f32[256,256]{1,0:T(8,128)S(1)}, f32[2,16,128]{2,1,0:T(8,128)S(1)}) custom-call(bf16[1024,4096]{1,0:T(8,128)(2,1)} %movie.1, bf16[4096,256]{1,0:T(8,128)(2,1)} %test.1), custom_call_target="tpu_custom_call" | custom-call | tf_op jit(solution)/shard_map/pallas_call | solution.py:355
  47.4 2.2 %shard_map.50 = (f32[1024,256]{1,0:T(8,128)}, f32[256,256]{1,0:T(8,128)}, f32[16,256]{1,0:T(8,128)}) custom-call(f32[1024,256]{1,0:T(8,128)S(1)} %get-tuple-element.10.refs_0_, f32[256,256]{1,0:T(8,128)S(1)} %get-tuple-element.11.refs_1_, f32[256,256]{1,0:T(8,128)S(1)} %get-tuple-element.12.refs_2_, f32[2,16,128]{2,1,0:T(8,128)S(1)} %get-tuple-element.13.refs_3_), custom_call_target="tpu_custom_call" | custom-call | tf_op jit(solution)/shard_map/pallas_call | solution.py:391

commit v3 on v2

v3 whole, which is shorter than its diff:
```python
import jax
import jax.numpy as jnp
from jax import lax
from jax.experimental import pallas as pl
from jax.experimental.pallas import tpu as pltpu
from jax.sharding import PartitionSpec as P

F = jnp.float32
HI = lax.Precision.HIGHEST
MESH = pl.DeviceIdType.MESH
VMEM = pltpu.VMEM
DMA = pltpu.SemaphoreType.DMA
NX, NZ, NY = 4, 8, 4
CHUNKS, WIDE, BLOCK, LAG, PIECES = 8, 512, 256, 4, 24


def place(x, z, y, s):
    return ((x * NZ + z) * NY + y, s)


def remote(src, dst, send, recv, device):
    return pltpu.make_async_remote_copy(
        src_ref=src, dst_ref=dst, send_sem=send, recv_sem=recv, device_id=device, device_id_type=MESH
    )


def each(lo, hi, body):
    lax.fori_loop(lo, hi, lambda i, c: (body(i), c)[1], 0)


def factor64(block, left):
    lane = lax.broadcasted_iota(jnp.int32, (8, 8, 128), 2)
    line = lax.broadcasted_iota(jnp.int32, (8, 8, 128), 0) * 8 + lax.broadcasted_iota(jnp.int32, (8, 8, 128), 1)
    sub = lax.broadcasted_iota(jnp.int32, (8, 128), 0)
    here = (lane < 64) if left else (lane >= 64)
    at, eye = (0, 64) if left else (64, 0)
    below = jnp.where(here, block.reshape(8, 8, 128), (lane == eye + line).astype(F))
    done = []
    for p in range(8):
        n = 8 - p
        first = at + 8 * p
        cols = [jnp.broadcast_to(below[:, :, first + j:first + j + 1], (n, 8, 128)) for j in range(8)]
        pivot = jnp.ones((8, 128), F)
        for k in range(8):
            d = jnp.broadcast_to(cols[k][0, k:k + 1, :], (8, 128))
            pivot = jnp.where(sub == k, d, pivot)
            m = cols[k] * (1.0 / d)[None]
            top = jnp.where(sub > k, m[0], 0.0)[None]
            m = jnp.concatenate([top, m[1:]], axis=0) if n > 1 else top
            row = jnp.broadcast_to(below[0, k:k + 1, :], (8, 128))
            for j in range(k + 1, 8):
                u = jnp.broadcast_to(cols[j][0, k:k + 1, :], (8, 128))
                cols[j] = cols[j] - m * u[None]
            below = below - m * row[None]
        done.append(lax.rsqrt(pivot) * below[0])
        below = below[1:]
    out = jnp.stack(done)
    return jnp.where(here & (lane - at < line), 0.0, out).reshape(64, 128)


def factor_block(t_ref, diag_ref, s):
    col = lax.broadcasted_iota(jnp.int32, (64, 256), 1)
    row = lax.broadcasted_iota(jnp.int32, (64, 256), 0)
    r0 = 64 * s
    tile = 128 * (s // 2)
    left = s % 2 == 0
    t = t_ref[r0 : r0 + 64, :]
    both = factor64(t[:, tile : tile + 128], left)
    diag_ref[r0 : r0 + 64, :] = both
    y = jnp.where((col >= r0) & (col < r0 + 64), (col - r0 == row).astype(F), t)
    z = jnp.zeros((64, 256), F)
    us = jnp.dot(both, jnp.concatenate([z, y] if left else [y, z], axis=0), precision=HI, preferred_element_type=F)
    t_ref[r0 : r0 + 64, :] = us
    if s < 3:
        full = lax.dot_general(us, us, (((0,), (0,)), ((), ())), precision=HI, preferred_element_type=F)
        col = lax.broadcasted_iota(jnp.int32, (192 - r0, 256), 1)
        rest = jnp.where((col >= r0) & (col < r0 + 64), 0.0, t_ref[r0 + 64 :, :])
        t_ref[r0 + 64 :, :] = rest - full[r0 + 64 :, :]


def parts(t_ref, diag_ref):
    col = lax.broadcasted_iota(jnp.int32, (256, 256), 1)
    row = lax.broadcasted_iota(jnp.int32, (256, 256), 0)
    t = t_ref[...]
    d = diag_ref[...]
    dd = jnp.concatenate([d, d], axis=1)
    upper = jnp.where(col // 64 == row // 64, dd, t)
    return jnp.where(col >= row, upper, 0.0), jnp.where(col <= row, t, 0.0)


def reduce_kernel(
    movie, test, pair, upper, inverse, cross,
    mv, tv, turned, grown, part, drecv, half, gpart, grs, gz, gram, t_ref, diag_ref,
    a_tmp, a_in, b_tmp, b_in, pa, pb, r2, p2, r3, p3,
    msem, tsem, dsend, drsem, gs_send, gs_recv, gz_send, gz_recv, ga_send, ga_recv,
    s1_send, s1_recv, s2_send, s2_recv, s3_send, s3_recv, s4_send, s4_recv,
):
    vox, s = lax.axis_index("vox"), lax.axis_index("sub")
    y = lax.rem(vox, NY)
    z = lax.rem(lax.div(vox, NY), NZ)
    x = lax.div(vox, NY * NZ)
    q = (x * NY + y) * 2 + s
    other = place(x, z, y, 1 - s)

    def block(b):
        return pl.ds(pl.multiple_of(b * BLOCK, BLOCK), BLOCK)

    def load(b):
        return pltpu.make_async_copy(movie.at[block(b)], mv.at[block(b)], msem.at[b])

    load_test = pltpu.make_async_copy(test, tv, tsem.at[0])
    load_test.start()
    each(0, 4, lambda b: load(b).start())

    def plane(d):
        t = lax.rem(q + d, 32)
        return t, place(lax.div(t, NY * 2), z, lax.rem(lax.div(t, 2), NY), lax.rem(t, 2))

    def column(d):
        t = lax.rem(z + d, NZ)
        return t, place(x, t, y, s)

    barrier = pltpu.get_barrier_semaphore()

    def greet(device):
        pl.semaphore_signal(barrier, inc=1, device_id=device, device_id_type=MESH)

    each(1, 32, lambda d: greet(plane(d)[1]))
    each(1, NZ, lambda d: greet(column(d)[1]))

    grown[...] = jnp.zeros_like(grown)
    load_test.wait()

    def project(b):
        load(b).wait()
        sketch = jnp.dot(mv[block(b)], tv[...], preferred_element_type=F)
        near = sketch.astype(jnp.bfloat16)
        both = jnp.concatenate([near, (sketch - near.astype(F)).astype(jnp.bfloat16)], axis=1)
        pair[block(b)] = both
        across = jnp.transpose(both)
        turned[:, block(b)] = across
        grown[...] += jnp.dot(across, both, preferred_element_type=F)

    each(0, 4, project)
    low, high = slice(0, 256), slice(256, 512)
    product = (grown[low, low] + grown[high, high]) + (grown[low, high] + grown[high, low])
    top, bottom = slice(0, 128), slice(128, 256)
    quarters = ((top, top), (top, bottom), (bottom, bottom))
    for i, (a, b) in enumerate(quarters):
        gpart[8 * i : 8 * i + 8] = product[a, b].reshape(8, 16, 128)

    xr, xo, xl = (lax.rem(x + d, NX) for d in (1, 2, 3))
    yr, yo, yl = (lax.rem(y + d, NY) for d in (1, 2, 3))
    right_x, left_x = place(xr, z, y, s), place(xl, z, y, s)
    right_y, left_y = place(x, z, yr, s), place(x, z, yl, s)

    turn = lax.rem(x + y, 4)
    owner = turn < 3
    mine = (x * 3 + lax.min(turn, 2)) * 2 + s

    def others(body):
        def visit(j):
            t = lax.rem(mine + j, PIECES)
            tx, ts = lax.div(t, 6), lax.rem(t, 2)
            ty = lax.rem(lax.rem(lax.div(t, 2), 3) - tx + 4, 4)
            at = (tx * NY + ty) * 2 + ts

            @pl.when(at != q)
            def _():
                body(t, at, place(tx, z, ty, ts))

        each(0, PIECES, visit)

    pl.semaphore_wait(barrier, 31 + NZ - 1)

    def gram_scatter(t, at, device):
        d = lax.rem(at - q + 32, 32)
        return remote(gpart.at[t], grs.at[d], gs_send.at[t], gs_recv.at[d], device)

    others(lambda *a: gram_scatter(*a).start())

    def across(i):
        rows = pl.ds(pl.multiple_of((1 - s) * 128, 128), 128)
        return remote(part.at[i, rows], drecv.at[i], dsend.at[i], drsem.at[i], other)

    def multiply(i):
        h, r = i // 4, i % 4
        first = pl.multiple_of((2 * lax.rem(xo + r, NX) + h) * WIDE, WIDE)
        part[i] = jnp.dot(turned[low], mv[:, pl.ds(first, WIDE)], preferred_element_type=F)
        across(i).start()

    be, af, every = pl.ds(0, 2), pl.ds(2, 2), pl.ds(0, 4)

    def ring(h, i, src, dst, device):
        return remote(src, dst, s1_send.at[h, i], s1_recv.at[h, i], device)

    ring_a = [
        [
            ring(h, 0, half.at[h, 0, be], a_tmp.at[h, 0], right_x),
            ring(h, 1, half.at[h, 0, af], a_tmp.at[h, 1], left_x),
            ring(h, 2, half.at[h, 3, af], a_in.at[h, 0, af], right_x),
            ring(h, 3, half.at[h, 1, be], a_in.at[h, 1, be], left_x),
            ring(h, 4, half.at[h, 3, be], a_in.at[h, 0, be], right_x),
            ring(h, 5, half.at[h, 1, af], a_in.at[h, 1, af], left_x),
        ]
        for h in range(2)
    ]
    ring_b = [
        [
            ring(h, 0, half.at[h, be, every, yo], b_tmp.at[h, 0], right_y),
            ring(h, 1, half.at[h, af, every, yo], b_tmp.at[h, 1], left_y),
            ring(h, 2, half.at[h, af, every, yr], b_in.at[h, 0, af], right_y),
            ring(h, 3, half.at[h, be, every, yl], b_in.at[h, 1, be], left_y),
            ring(h, 4, half.at[h, be, every, yr], b_in.at[h, 0, be], right_y),
            ring(h, 5, half.at[h, af, every, yl], b_in.at[h, 1, af], left_y),
        ]
        for h in range(2)
    ]

    def begin(h, a, b):
        @pl.when(s == 0)
        def _():
            for i in a:
                ring_a[h][i].start()

        @pl.when(s == 1)
        def _():
            for i in b:
                ring_b[h][i].start()

    after = {0: ((0, 1), ()), 1: ((3,), (0, 3)), 3: ((2,), (1, 2))}
    for step in range(CHUNKS + LAG):
        if step < CHUNKS:
            multiply(step)
        i = step - LAG
        if i >= 0:
            across(i).wait_recv()
            both = part[i, pl.ds(pl.multiple_of(s * 128, 128), 128)] + drecv[i]
            half[i // 4, i % 4] = jnp.transpose(both).reshape(4, NY, 32, 128)
            if i % 4 in after:
                begin(i // 4, *after[i % 4])

    def ring_again(h):
        @pl.when(s == 0)
        def _():
            ring_a[h][0].wait_recv()
            half[h, 3, be] = half[h, 3, be] + a_tmp[h, 0]
            ring_a[h][4].start()
            ring_a[h][1].wait_recv()
            half[h, 1, af] = half[h, 1, af] + a_tmp[h, 1]
            ring_a[h][5].start()

        @pl.when(s == 1)
        def _():
            ring_b[h][0].wait_recv()
            half[h, be, every, yr] = half[h, be, every, yr] + b_tmp[h, 0]
            ring_b[h][4].start()
            ring_b[h][1].wait_recv()
            half[h, af, every, yl] = half[h, af, every, yl] + b_tmp[h, 1]
            ring_b[h][5].start()

    def second_a(h, d):
        t = (yr, yo, yl)[d]
        return remote(pa.at[h, every, t], r2.at[h, d], s2_send.at[h, d], s2_recv.at[h, d], place(x, z, t, s))

    def second_b(h, d):
        t = (xr, xo, xl)[d]
        return remote(pb.at[h, (3, 0, 1)[d]], r2.at[h, d], s2_send.at[h, d], s2_recv.at[h, d], place(t, z, y, s))

    def second(h):
        @pl.when(s == 0)
        def _():
            for copy in ring_a[h][2:]:
                copy.wait_recv()
            pa[h] = half[h, 2] + a_in[h, 0] + a_in[h, 1]
            for d in range(3):
                second_a(h, d).start()

        @pl.when(s == 1)
        def _():
            for copy in ring_b[h][2:]:
                copy.wait_recv()
            pb[h] = half[h, :, :, y] + b_in[h, 0] + b_in[h, 1]
            for d in range(3):
                second_b(h, d).start()

    def third(d):
        t, device = column(d)
        return remote(p2.at[t], r3.at[d], s3_send.at[d], s3_recv.at[d], device)

    def third_start(h):
        for d in range(3):
            second_a(h, d).wait_recv()

        @pl.when(s == 0)
        def _():
            p2[4 * h : 4 * h + 4] = pa[h, :, y] + r2[h, 0] + r2[h, 1] + r2[h, 2]

        @pl.when(s == 1)
        def _():
            p2[4 * h : 4 * h + 4] = pb[h, 2] + r2[h, 0] + r2[h, 1] + r2[h, 2]

        def visit(d):
            @pl.when(lax.div(column(d)[0], 4) == h)
            def _():
                third(d).start()

        each(1, NZ, visit)

    def gram_column(d):
        t, device = column(d)
        return remote(gz.at[z], gz.at[z], gz_send.at[d], gz_recv.at[d], device)

    def gram_column_from(d):
        t = lax.rem(z - d + NZ, NZ)
        return remote(gz.at[t], gz.at[t], gz_send.at[d], gz_recv.at[d], place(x, t, y, s))

    def gram_gather(d):
        return remote(gram.at[mine], gram.at[mine], ga_send.at[d], ga_recv.at[mine], plane(d)[1])

    def gram_gather_from(t, at, device):
        return remote(gram.at[t], gram.at[t], ga_send.at[0], ga_recv.at[t], device)

    ring_again(0)

    @pl.when(owner)
    def _():
        each(1, 32, lambda d: remote(gpart.at[0], grs.at[d], gs_send.at[0], gs_recv.at[d], other).wait_recv())
        total = gpart[mine]
        for d in range(1, 32):
            total = total + grs[d]
        gz[z] = total
        each(1, NZ, lambda d: gram_column(d).start())

    ring_again(1)
    second(0)

    @pl.when(owner)
    def _():
        each(1, NZ, lambda d: gram_column_from(d).wait_recv())
        each(1, NZ, lambda d: gram_column(d).wait_send())
        total = gz[0]
        for j in range(1, NZ):
            total = total + gz[j]
        gram[mine] = total
        each(1, 32, lambda d: gram_gather(d).start())

    second(1)
    third_start(0)
    third_start(1)

    others(lambda *a: gram_gather_from(*a).wait_recv())
    t_ref[bottom, top] = jnp.zeros((128, 128), F)
    for i, (a, b) in enumerate(quarters):
        t_ref[a, b] = gram[8 * i : 8 * i + 8].reshape(128, 128)
    for block in range(4):
        factor_block(t_ref, diag_ref, block)
    upper[...], inverse[...] = parts(t_ref, diag_ref)

    each(1, NZ, lambda d: third(d).wait_recv())
    total = p2[z]
    for d in range(1, NZ):
        total = total + r3[d]
    p3[...] = total.reshape(2, 16, 128)
    last = remote(p3.at[1 - s], cross.at[s], s4_send.at[0], s4_recv.at[0], other)
    last.start()
    cross[s] = p3[s]
    remote(p3.at[s], cross.at[1 - s], s4_send.at[0], s4_recv.at[0], other).wait_recv()

    others(lambda *a: gram_scatter(*a).wait_send())

    @pl.when(owner)
    def _():
        each(1, 32, lambda d: gram_gather(d).wait_send())

    each(0, CHUNKS, lambda i: across(i).wait_send())
    each(1, NZ, lambda d: third(d).wait_send())
    last.wait_send()

    @pl.when(s == 0)
    def _():
        for h in range(2):
            for copy in ring_a[h]:
                copy.wait_send()
            for d in range(3):
                second_a(h, d).wait_send()

    @pl.when(s == 1)
    def _():
        for h in range(2):
            for copy in ring_b[h]:
                copy.wait_send()
            for d in range(3):
                second_b(h, d).wait_send()


def finish_kernel(voxels, pair, upper, inverse, cross, basis, r_factor, projected):
    scale = jnp.sqrt(F(voxels))
    turned = jnp.transpose(inverse[...])
    scaled = turned * scale
    near = scaled.astype(jnp.bfloat16)
    rest = (scaled - near.astype(F)).astype(jnp.bfloat16)
    basis[...] = jnp.dot(pair[...], jnp.concatenate([near, near], axis=0), preferred_element_type=F) + jnp.dot(
        pair[:, :256], rest, preferred_element_type=F
    )
    r_factor[...] = upper[...] / scale
    both = jnp.concatenate([cross[0], cross[1]], axis=1)
    projected[...] = jnp.dot(both, turned, precision=HI, preferred_element_type=F)


def local(movie, test_matrix):
    shape = jax.ShapeDtypeStruct
    movie, test_matrix = (pltpu.with_memory_space_constraint(a, pltpu.HBM) for a in (movie, test_matrix))
    in_vmem = pl.BlockSpec(memory_space=VMEM)
    square = shape((256, 256), F)
    pair, upper, inverse, cross = pl.pallas_call(
        reduce_kernel,
        out_shape=(shape((1024, 512), jnp.bfloat16), square, square, shape((2, 16, 128), F)),
        in_specs=[pl.BlockSpec(memory_space=pltpu.HBM)] * 2,
        out_specs=[in_vmem] * 4,
        scratch_shapes=[
            VMEM((1024, 4096), jnp.bfloat16),
            VMEM((4096, 256), jnp.bfloat16),
            VMEM((512, 1024), jnp.bfloat16),
            VMEM((512, 512), F),
            VMEM((CHUNKS, 256, WIDE), F),
            VMEM((CHUNKS, 128, WIDE), F),
            VMEM((2, NX, 4, NY, 32, 128), F),
            VMEM((PIECES, 16, 128), F),
            VMEM((32, 16, 128), F),
            VMEM((NZ, 16, 128), F),
            VMEM((PIECES, 16, 128), F),
            VMEM((256, 256), F),
            VMEM((256, 128), F),
            VMEM((2, 2, 2, NY, 32, 128), F),
            VMEM((2, 2, 4, NY, 32, 128), F),
            VMEM((2, 2, 2, 4, 32, 128), F),
            VMEM((2, 2, NX, 4, 32, 128), F),
            VMEM((2, 4, NY, 32, 128), F),
            VMEM((2, NX, 4, 32, 128), F),
            VMEM((2, 3, 4, 32, 128), F),
            VMEM((NZ, 32, 128), F),
            VMEM((NZ, 32, 128), F),
            VMEM((2, 16, 128), F),
        ]
        + [DMA((n,)) for n in (4, 1, 8, 8, PIECES, 32, 8, 8, 32, PIECES)]
        + [DMA(n) for n in ((2, 6), (2, 6), (2, 3), (2, 3), (8,), (8,), (1,), (1,))],
        compiler_params=pltpu.CompilerParams(
            collective_id=0, has_side_effects=True, vmem_limit_bytes=40 * 1024 * 1024
        ),
    )(movie, test_matrix)
    voxels = movie.shape[0] * NX * NY * NZ * 2
    basis, r_factor, projected = pl.pallas_call(
        lambda *refs: finish_kernel(voxels, *refs),
        out_shape=(shape((1024, 256), F), square, shape((16, 256), F)),
        in_specs=[in_vmem] * 4,
        out_specs=[in_vmem] * 3,
        compiler_params=pltpu.CompilerParams(vmem_limit_bytes=16 * 1024 * 1024),
    )(pair, upper, inverse, cross)
    return basis, r_factor, projected.T


def solution(mesh):
    placed = (P(("vox", "sub"), None), P())
    return jax.shard_map(
        local,
        mesh=mesh,
        in_specs=placed,
        out_specs=(P(("vox", "sub"), None), P(), P(None, ("vox", "sub"))),
        check_vma=False,
    )
```

time: 49.7 us -> 52 us (1.046)
  Pallas kernels: 49 us -> 51.3 us
    pallas_call x1, Pallas kernels: 46.8 us -> 49.5 us  [local(): pl.pallas_call(reduce_kernel, out_shape=(shape((1024, 512), jnp.bfloat16)...]
where the time goes in v3:
time: 52 us; the launch traced here: 51.9 us
  Pallas kernels  51.3 us (99%)
  between operations  0.64 us (1%)
    pallas_call x1, Pallas kernels, local(): pl.pallas_call(reduce_kernel, out_shape=(shape((1024, 512), jnp.bfloat16)...  49.5 us
    pallas_call x1, Pallas kernels, local(): pl.pallas_call(lambda *refs: finish_kernel(voxels, *refs), out_shape=(sha...  1.78 us

profile of v3, /device:TPU:1, one launch (start us, length us, event | category | flops | bytes accessed | tf_op | source)
XLA Modules:
  0.0 51.9 jit_solution(11666594291296627650)
XLA Ops:
  0.6 49.5 %shard_map.49 = (bf16[1024,512]{1,0:T(8,128)(2,1)S(1)}, f32[256,256]{1,0:T(8,128)S(1)}, f32[256,256]{1,0:T(8,128)S(1)}, f32[2,16,128]{2,1,0:T(8,128)S(1)}) custom-call(bf16[1024,4096]{1,0:T(8,128)(2,1)} %movie.1, bf16[4096,256]{1,0:T(8,128)(2,1)} %test.1), custom_call_target="tpu_custom_call" | custom-call | tf_op jit(solution)/shard_map/pallas_call | solution.py:416
  50.2 1.8 %shard_map.50 = (f32[1024,256]{1,0:T(8,128)}, f32[256,256]{1,0:T(8,128)}, f32[16,256]{1,0:T(8,128)}) custom-call(bf16[1024,512]{1,0:T(8,128)(2,1)S(1)} %get-tuple-element.10.refs_0_, f32[256,256]{1,0:T(8,128)S(1)} %get-tuple-element.11.refs_1_, f32[256,256]{1,0:T(8,128)S(1)} %get-tuple-element.12.refs_2_, f32[2,16,128]{2,1,0:T(8,128)S(1)} %get-tuple-element.13.refs_3_), custom_call_target="tpu_custom_call" | custom-call | tf_op jit(solution)/shard_map/pallas_call | solution.py:453

commit v4 on v3

--- a/solution.py
+++ b/solution.py
@@ -11,7 +11,7 @@
 VMEM = pltpu.VMEM
 DMA = pltpu.SemaphoreType.DMA
 NX, NZ, NY = 4, 8, 4
-CHUNKS, WIDE, BLOCK, LAG, PIECES = 8, 512, 256, 4, 24
+CHUNKS, WIDE, LAG, PIECES = 8, 512, 4, 24
 
 
 def place(x, z, y, s):
@@ -90,7 +90,7 @@
 
 def reduce_kernel(
     movie, test, pair, upper, inverse, cross,
-    mv, tv, turned, grown, part, drecv, half, gpart, grs, gz, gram, t_ref, diag_ref,
+    mv, tv, sketch, turned, grown, part, drecv, half, gpart, grs, gz, gram, t_ref, diag_ref,
     a_tmp, a_in, b_tmp, b_in, pa, pb, r2, p2, r3, p3,
     msem, tsem, dsend, drsem, gs_send, gs_recv, gz_send, gz_recv, ga_send, ga_recv,
     s1_send, s1_recv, s2_send, s2_recv, s3_send, s3_recv, s4_send, s4_recv,
@@ -102,15 +102,18 @@
     q = (x * NY + y) * 2 + s
     other = place(x, z, y, 1 - s)
 
-    def block(b):
-        return pl.ds(pl.multiple_of(b * BLOCK, BLOCK), BLOCK)
-
-    def load(b):
-        return pltpu.make_async_copy(movie.at[block(b)], mv.at[block(b)], msem.at[b])
-
-    load_test = pltpu.make_async_copy(test, tv, tsem.at[0])
-    load_test.start()
-    each(0, 4, lambda b: load(b).start())
+    def load(c):
+        wide = pl.ds(pl.multiple_of(c * WIDE, WIDE), WIDE)
+        return (
+            pltpu.make_async_copy(movie.at[:, wide], mv.at[c], msem.at[c]),
+            pltpu.make_async_copy(test.at[wide], tv.at[c], tsem.at[c]),
+        )
+
+    def start(c):
+        for copy in load(c):
+            copy.start()
+
+    each(0, CHUNKS, start)
 
     def plane(d):
         t = lax.rem(q + d, 32)
@@ -128,20 +131,18 @@
     each(1, 32, lambda d: greet(plane(d)[1]))
     each(1, NZ, lambda d: greet(column(d)[1]))
 
-    grown[...] = jnp.zeros_like(grown)
-    load_test.wait()
-
-    def project(b):
-        load(b).wait()
-        sketch = jnp.dot(mv[block(b)], tv[...], preferred_element_type=F)
-        near = sketch.astype(jnp.bfloat16)
-        both = jnp.concatenate([near, (sketch - near.astype(F)).astype(jnp.bfloat16)], axis=1)
-        pair[block(b)] = both
-        across = jnp.transpose(both)
-        turned[:, block(b)] = across
-        grown[...] += jnp.dot(across, both, preferred_element_type=F)
-
-    each(0, 4, project)
+    sketch[...] = jnp.zeros_like(sketch)
+
+    def project(c):
+        for copy in load(c):
+            copy.wait()
+        sketch[...] += jnp.dot(mv[c], tv[c], preferred_element_type=F)
+
+    each(0, CHUNKS, project)
+    near = sketch[...].astype(jnp.bfloat16)
+    pair[...] = jnp.concatenate([near, (sketch[...] - near.astype(F)).astype(jnp.bfloat16)], axis=1)
+    turned[...] = jnp.transpose(pair[...])
+    grown[...] = jnp.dot(turned[...], pair[...], preferred_element_type=F)
     low, high = slice(0, 256), slice(256, 512)
     product = (grown[low, low] + grown[high, high]) + (grown[low, high] + grown[high, low])
     top, bottom = slice(0, 128), slice(128, 256)
@@ -185,8 +186,8 @@
 
     def multiply(i):
         h, r = i // 4, i % 4
-        first = pl.multiple_of((2 * lax.rem(xo + r, NX) + h) * WIDE, WIDE)
-        part[i] = jnp.dot(turned[low], mv[:, pl.ds(first, WIDE)], preferred_element_type=F)
+        chunk = 2 * lax.rem(xo + r, NX) + h
+        part[i] = jnp.dot(turned[low], mv[chunk], preferred_element_type=F)
         across(i).start()
 
     be, af, every = pl.ds(0, 2), pl.ds(2, 2), pl.ds(0, 4)
@@ -321,40 +322,48 @@
     def gram_gather_from(t, at, device):
         return remote(gram.at[t], gram.at[t], ga_send.at[0], ga_recv.at[t], device)
 
+    def gram_pieces():
+        @pl.when(owner)
+        def _():
+            each(1, 32, lambda d: remote(gpart.at[0], grs.at[d], gs_send.at[0], gs_recv.at[d], other).wait_recv())
+            total = gpart[mine]
+            for d in range(1, 32):
+                total = total + grs[d]
+            gz[z] = total
+            each(1, NZ, lambda d: gram_column(d).start())
+
+    def gram_totals():
+        @pl.when(owner)
+        def _():
+            each(1, NZ, lambda d: gram_column_from(d).wait_recv())
+            each(1, NZ, lambda d: gram_column(d).wait_send())
+            total = gz[0]
+            for j in range(1, NZ):
+                total = total + gz[j]
+            gram[mine] = total
+            each(1, 32, lambda d: gram_gather(d).start())
+
+    def gram_whole():
+        others(lambda *a: gram_gather_from(*a).wait_recv())
+        t_ref[bottom, top] = jnp.zeros((128, 128), F)
+        for i, (a, b) in enumerate(quarters):
+            t_ref[a, b] = gram[8 * i : 8 * i + 8].reshape(128, 128)
+
+    def factor(block):
+        factor_block(t_ref, diag_ref, block)
+
+    gram_pieces()
     ring_again(0)
-
-    @pl.when(owner)
-    def _():
-        each(1, 32, lambda d: remote(gpart.at[0], grs.at[d], gs_send.at[0], gs_recv.at[d], other).wait_recv())
-        total = gpart[mine]
-        for d in range(1, 32):
-            total = total + grs[d]
-        gz[z] = total
-        each(1, NZ, lambda d: gram_column(d).start())
-
     ring_again(1)
+    gram_totals()
     second(0)
-
-    @pl.when(owner)
-    def _():
-        each(1, NZ, lambda d: gram_column_from(d).wait_recv())
-        each(1, NZ, lambda d: gram_column(d).wait_send())
-        total = gz[0]
-        for j in range(1, NZ):
-            total = total + gz[j]
-        gram[mine] = total
-        each(1, 32, lambda d: gram_gather(d).start())
-
     second(1)
     third_start(0)
+    gram_whole()
+    factor(0)
     third_start(1)
-
-    others(lambda *a: gram_gather_from(*a).wait_recv())
-    t_ref[bottom, top] = jnp.zeros((128, 128), F)
-    for i, (a, b) in enumerate(quarters):
-        t_ref[a, b] = gram[8 * i : 8 * i + 8].reshape(128, 128)
-    for block in range(4):
-        factor_block(t_ref, diag_ref, block)
+    for block in range(1, 4):
+        factor(block)
     upper[...], inverse[...] = parts(t_ref, diag_ref)
 
     each(1, NZ, lambda d: third(d).wait_recv())
@@ -419,8 +428,9 @@
         in_specs=[pl.BlockSpec(memory_space=pltpu.HBM)] * 2,
         out_specs=[in_vmem] * 4,
         scratch_shapes=[
-            VMEM((1024, 4096), jnp.bfloat16),
-            VMEM((4096, 256), jnp.bfloat16),
+            VMEM((CHUNKS, 1024, WIDE), jnp.bfloat16),
+            VMEM((CHUNKS, WIDE, 256), jnp.bfloat16),
+            VMEM((1024, 256), F),
             VMEM((512, 1024), jnp.bfloat16),
             VMEM((512, 512), F),
             VMEM((CHUNKS, 256, WIDE), F),
@@ -443,7 +453,7 @@
             VMEM((NZ, 32, 128), F),
             VMEM((2, 16, 128), F),
         ]
-        + [DMA((n,)) for n in (4, 1, 8, 8, PIECES, 32, 8, 8, 32, PIECES)]
+        + [DMA((n,)) for n in (8, 8, 8, 8, PIECES, 32, 8, 8, 32, PIECES)]
         + [DMA(n) for n in ((2, 6), (2, 6), (2, 3), (2, 3), (8,), (8,), (1,), (1,))],
         compiler_params=pltpu.CompilerParams(
             collective_id=0, has_side_effects=True, vmem_limit_bytes=40 * 1024 * 1024

time: 52 us -> 48.9 us (0.940)
  Pallas kernels: 51.3 us -> 48.2 us
    pallas_call x1, Pallas kernels: 49.5 us -> 46.4 us  [local(): pl.pallas_call(reduce_kernel, out_shape=(shape((1024, 512), jnp.bfloat16)...]
where the time goes in v4:
time: 48.9 us; the launch traced here: 48.8 us
  Pallas kernels  48.2 us (99%)
  between operations  0.64 us (1%)
    pallas_call x1, Pallas kernels, local(): pl.pallas_call(reduce_kernel, out_shape=(shape((1024, 512), jnp.bfloat16)...  46.4 us
    pallas_call x1, Pallas kernels, local(): pl.pallas_call(lambda *refs: finish_kernel(voxels, *refs), out_shape=(sha...  1.78 us

profile of v4, /device:TPU:1, one launch (start us, length us, event | category | flops | bytes accessed | tf_op | source)
XLA Modules:
  0.0 48.8 jit_solution(10356049720624770583)
XLA Ops:
  0.6 46.4 %shard_map.49 = (bf16[1024,512]{1,0:T(8,128)(2,1)S(1)}, f32[256,256]{1,0:T(8,128)S(1)}, f32[256,256]{1,0:T(8,128)S(1)}, f32[2,16,128]{2,1,0:T(8,128)S(1)}) custom-call(bf16[1024,4096]{1,0:T(8,128)(2,1)} %movie.1, bf16[4096,256]{1,0:T(8,128)(2,1)} %test.1), custom_call_target="tpu_custom_call" | custom-call | tf_op jit(solution)/shard_map/pallas_call | solution.py:425
  47.0 1.8 %shard_map.50 = (f32[1024,256]{1,0:T(8,128)}, f32[256,256]{1,0:T(8,128)}, f32[16,256]{1,0:T(8,128)}) custom-call(bf16[1024,512]{1,0:T(8,128)(2,1)S(1)} %get-tuple-element.10.refs_0_, f32[256,256]{1,0:T(8,128)S(1)} %get-tuple-element.11.refs_1_, f32[256,256]{1,0:T(8,128)S(1)} %get-tuple-element.12.refs_2_, f32[2,16,128]{2,1,0:T(8,128)S(1)} %get-tuple-element.13.refs_3_), custom_call_target="tpu_custom_call" | custom-call | tf_op jit(solution)/shard_map/pallas_call | solution.py:463

commit v5 on v4

--- a/solution.py
+++ b/solution.py
@@ -28,69 +28,71 @@
     lax.fori_loop(lo, hi, lambda i, c: (body(i), c)[1], 0)
 
 
-def factor64(block, left):
-    lane = lax.broadcasted_iota(jnp.int32, (8, 8, 128), 2)
-    line = lax.broadcasted_iota(jnp.int32, (8, 8, 128), 0) * 8 + lax.broadcasted_iota(jnp.int32, (8, 8, 128), 1)
+def factor128(block, midway=None):
+    lane = lax.broadcasted_iota(jnp.int32, (8, 128), 1)
     sub = lax.broadcasted_iota(jnp.int32, (8, 128), 0)
-    here = (lane < 64) if left else (lane >= 64)
-    at, eye = (0, 64) if left else (64, 0)
-    below = jnp.where(here, block.reshape(8, 8, 128), (lane == eye + line).astype(F))
-    done = []
-    for p in range(8):
-        n = 8 - p
-        first = at + 8 * p
-        cols = [jnp.broadcast_to(below[:, :, first + j:first + j + 1], (n, 8, 128)) for j in range(8)]
+    below = block.reshape(16, 8, 128)
+    uppers, inverses = [], []
+    for p in range(16):
+        if p == 3 and midway is not None:
+            midway()
+        n, first = 16 - p, 8 * p
+        cols = [jnp.broadcast_to(below[:, :, first + j : first + j + 1], (n, 8, 128)) for j in range(8)]
+        inside = (lane >= first) & (lane < first + 8)
+        here = jnp.where(inside, (lane - first == sub).astype(F), below[0])[None]
+        if n > 1:
+            below = jnp.concatenate([here, jnp.where(inside[None], 0.0, below[1:])], axis=0)
+        else:
+            below = here
         pivot = jnp.ones((8, 128), F)
         for k in range(8):
-            d = jnp.broadcast_to(cols[k][0, k:k + 1, :], (8, 128))
+            d = jnp.broadcast_to(cols[k][0, k : k + 1, :], (8, 128))
             pivot = jnp.where(sub == k, d, pivot)
             m = cols[k] * (1.0 / d)[None]
             top = jnp.where(sub > k, m[0], 0.0)[None]
             m = jnp.concatenate([top, m[1:]], axis=0) if n > 1 else top
-            row = jnp.broadcast_to(below[0, k:k + 1, :], (8, 128))
+            row = jnp.broadcast_to(below[0, k : k + 1, :], (8, 128))
             for j in range(k + 1, 8):
-                u = jnp.broadcast_to(cols[j][0, k:k + 1, :], (8, 128))
+                u = jnp.broadcast_to(cols[j][0, k : k + 1, :], (8, 128))
                 cols[j] = cols[j] - m * u[None]
             below = below - m * row[None]
-        done.append(lax.rsqrt(pivot) * below[0])
+        upper = jnp.where(lane < first + 8, 0.0, below[0])
+        for j in range(8):
+            upper = jnp.where((lane == first + j) & (sub <= j), cols[j][0], upper)
+        scale = lax.rsqrt(pivot)
+        uppers.append(scale * upper)
+        inverses.append(scale * jnp.where(lane < first + 8, below[0], 0.0))
         below = below[1:]
-    out = jnp.stack(done)
-    return jnp.where(here & (lane - at < line), 0.0, out).reshape(64, 128)
-
-
-def factor_block(t_ref, diag_ref, s):
-    col = lax.broadcasted_iota(jnp.int32, (64, 256), 1)
-    row = lax.broadcasted_iota(jnp.int32, (64, 256), 0)
-    r0 = 64 * s
-    tile = 128 * (s // 2)
-    left = s % 2 == 0
-    t = t_ref[r0 : r0 + 64, :]
-    both = factor64(t[:, tile : tile + 128], left)
-    diag_ref[r0 : r0 + 64, :] = both
-    y = jnp.where((col >= r0) & (col < r0 + 64), (col - r0 == row).astype(F), t)
-    z = jnp.zeros((64, 256), F)
-    us = jnp.dot(both, jnp.concatenate([z, y] if left else [y, z], axis=0), precision=HI, preferred_element_type=F)
-    t_ref[r0 : r0 + 64, :] = us
-    if s < 3:
-        full = lax.dot_general(us, us, (((0,), (0,)), ((), ())), precision=HI, preferred_element_type=F)
-        col = lax.broadcasted_iota(jnp.int32, (192 - r0, 256), 1)
-        rest = jnp.where((col >= r0) & (col < r0 + 64), 0.0, t_ref[r0 + 64 :, :])
-        t_ref[r0 + 64 :, :] = rest - full[r0 + 64 :, :]
-
-
-def parts(t_ref, diag_ref):
-    col = lax.broadcasted_iota(jnp.int32, (256, 256), 1)
-    row = lax.broadcasted_iota(jnp.int32, (256, 256), 0)
-    t = t_ref[...]
-    d = diag_ref[...]
-    dd = jnp.concatenate([d, d], axis=1)
-    upper = jnp.where(col // 64 == row // 64, dd, t)
-    return jnp.where(col >= row, upper, 0.0), jnp.where(col <= row, t, 0.0)
+    return jnp.concatenate(uppers, axis=0), jnp.concatenate(inverses, axis=0)
+
+
+def times(a, b, turn=False):
+    return lax.dot_general(a, b, (((0 if turn else 1,), (0,)), ((), ())), precision=HI, preferred_element_type=F)
+
+
+def factor_first(t_ref, upper, inverse, midway=None):
+    top, bottom = slice(0, 128), slice(128, 256)
+    u, inv = factor128(t_ref[top, top], midway)
+    side = times(inv, t_ref[top, bottom])
+    t_ref[bottom, bottom] = t_ref[bottom, bottom] - times(side, side, True)
+    upper[top, top] = u
+    upper[top, bottom] = side
+    inverse[top, top] = inv
+    inverse[top, bottom] = jnp.zeros((128, 128), F)
+
+
+def factor_last(t_ref, upper, inverse):
+    top, bottom = slice(0, 128), slice(128, 256)
+    u, inv = factor128(t_ref[bottom, bottom])
+    upper[bottom, bottom] = u
+    upper[bottom, top] = jnp.zeros((128, 128), F)
+    inverse[bottom, bottom] = inv
+    inverse[bottom, top] = -times(inv, times(upper[top, bottom], inverse[top, top], True))
 
 
 def reduce_kernel(
     movie, test, pair, upper, inverse, cross,
-    mv, tv, sketch, turned, grown, part, drecv, half, gpart, grs, gz, gram, t_ref, diag_ref,
+    mv, tv, sketch, turned, grown, part, drecv, half, gpart, grs, gz, gram, t_ref,
     a_tmp, a_in, b_tmp, b_in, pa, pb, r2, p2, r3, p3,
     msem, tsem, dsend, drsem, gs_send, gs_recv, gz_send, gz_recv, ga_send, ga_recv,
     s1_send, s1_recv, s2_send, s2_recv, s3_send, s3_recv, s4_send, s4_recv,
@@ -345,12 +347,8 @@
 
     def gram_whole():
         others(lambda *a: gram_gather_from(*a).wait_recv())
-        t_ref[bottom, top] = jnp.zeros((128, 128), F)
         for i, (a, b) in enumerate(quarters):
             t_ref[a, b] = gram[8 * i : 8 * i + 8].reshape(128, 128)
-
-    def factor(block):
-        factor_block(t_ref, diag_ref, block)
 
     gram_pieces()
     ring_again(0)
@@ -360,11 +358,8 @@
     second(1)
     third_start(0)
     gram_whole()
-    factor(0)
-    third_start(1)
-    for block in range(1, 4):
-        factor(block)
-    upper[...], inverse[...] = parts(t_ref, diag_ref)
+    factor_first(t_ref, upper, inverse, lambda: third_start(1))
+    factor_last(t_ref, upper, inverse)
 
     each(1, NZ, lambda d: third(d).wait_recv())
     total = p2[z]
@@ -441,7 +436,6 @@
             VMEM((NZ, 16, 128), F),
             VMEM((PIECES, 16, 128), F),
             VMEM((256, 256), F),
-            VMEM((256, 128), F),
             VMEM((2, 2, 2, NY, 32, 128), F),
             VMEM((2, 2, 4, NY, 32, 128), F),
             VMEM((2, 2, 2, 4, 32, 128), F),

time: 48.9 us -> 48.5 us (level)
  no operation moved by 1% of the time
where the time goes in v5:
time: 48.5 us; the launch traced here: 48.4 us
  Pallas kernels  47.8 us (99%)
  between operations  0.64 us (1%)
    pallas_call x1, Pallas kernels, local(): pl.pallas_call(reduce_kernel, out_shape=(shape((1024, 512), jnp.bfloat16)...  46 us
    pallas_call x1, Pallas kernels, local(): pl.pallas_call(lambda *refs: finish_kernel(voxels, *refs), out_shape=(sha...  1.78 us

profile of v5, /device:TPU:1, one launch (start us, length us, event | category | flops | bytes accessed | tf_op | source)
XLA Modules:
  0.0 48.4 jit_solution(8532428569896741415)
XLA Ops:
  0.6 46.0 %shard_map.49 = (bf16[1024,512]{1,0:T(8,128)(2,1)S(1)}, f32[256,256]{1,0:T(8,128)S(1)}, f32[256,256]{1,0:T(8,128)S(1)}, f32[2,16,128]{2,1,0:T(8,128)S(1)}) custom-call(bf16[1024,4096]{1,0:T(8,128)(2,1)} %movie.1, bf16[4096,256]{1,0:T(8,128)(2,1)} %test.1), custom_call_target="tpu_custom_call" | custom-call | tf_op jit(solution)/shard_map/pallas_call | solution.py:420
  46.6 1.8 %shard_map.50 = (f32[1024,256]{1,0:T(8,128)}, f32[256,256]{1,0:T(8,128)}, f32[16,256]{1,0:T(8,128)}) custom-call(bf16[1024,512]{1,0:T(8,128)(2,1)S(1)} %get-tuple-element.10.refs_0_, f32[256,256]{1,0:T(8,128)S(1)} %get-tuple-element.11.refs_1_, f32[256,256]{1,0:T(8,128)S(1)} %get-tuple-element.12.refs_2_, f32[2,16,128]{2,1,0:T(8,128)S(1)} %get-tuple-element.13.refs_3_), custom_call_target="tpu_custom_call" | custom-call | tf_op jit(solution)/shard_map/pallas_call | solution.py:457
